TPU v7x, 32 devices: a whole 2x2x4 slice. The times are simulated.
32 devices in a mesh: gx: 4 (over z), gy: 4 (over y, x), gz: 2 (over core).
Axes of the slice: x: 2, y: 2, z: 4, core: 2. Of those that a mesh axis runs over, the one named last changes fastest.
Arguments:
- forces: float32 [3, 64, 64, 256], P(None, 'gx', 'gy', 'gz'), may hold values from -8 to 8
- mass_shift: float32 [64, 64, 256], P('gx', 'gy', 'gz'), may hold values from 0.5 to 2
- deflation: float32 [16, 3, 64, 64, 256], P(None, None, 'gx', 'gy', 'gz'), may hold values from -0.01953125 to 0.01953125
- coarse_factor: float32 [512, 512], P('gz'), may hold values from -0.041033009 to 0.6, as said below
- coarse_slot: int32 [32], replicated, may hold values from 0 to 31, each once
Outputs:
- solution: float32 [3, 64, 64, 256], P(None, 'gx', 'gy', 'gz')
- residual: float32 [3, 64, 64, 256], P(None, 'gx', 'gy', 'gz')
- direction: float32 [3, 64, 64, 256], P(None, 'gx', 'gy', 'gz')
Inputs may be any that keep to these rules, and one draw needn't show every extreme that they name: `coarse_factor`: lower triangular: zero above the diagonal; diagonal entries between 0.3 and 0.6. `coarse_slot`: each subdomain has its own coarse position.
All inputs are finite; a program needn't handle non-finite values.
Results may differ from a plain program's by a relative error of at most 0.0003.
Values sent between devices are 32-bit elements; how exact they have to be, the bound alone decides.
A program may use at most 192 MiB of HBM per device.

v0:
```python
import functools

import jax
import jax.numpy as jnp
from jax import lax
from jax.experimental import pallas as pl
from jax.experimental.pallas import tpu as pltpu
from jax.sharding import PartitionSpec as P

SWEEPS = 3
ITERS = 4
MESH = pl.DeviceIdType.MESH
HIGHEST = lax.Precision.HIGHEST
W = 3
LEAD = 4
DIRS = tuple((dx, dy) for dx in (-1, 0, 1) for dy in (-1, 0, 1) if (dx, dy) != (0, 0))
BLOCK = 128


def dot(a, b):
    return jnp.dot(a, b, precision=HIGHEST, preferred_element_type=jnp.float32)


def kernel(
    sizes,
    forces, mass, defl_hbm, factor, slot_column,
    sol, res, direc,
    zext, rext, idir, cext, mext, cor, ua, ub, uz, vx,
    low, high, got_low, got_high,
    low_c, high_c, got_low_c, got_high_c,
    low_m, high_m, got_low_m, got_high_m,
    zsend, zgot, vzb, defl,
    full, inv, sol_mat, gsend, gat, gres, gdir,
    zx_send, zx_recv, c_send, c_recv, m_send, m_recv,
    zc_send, zc_recv, g_send, g_recv, f_send, f_recv, f_local, d_local,
):
    nx, ny, nz, cx, cy, vectors, order = sizes
    n = nx * ny * nz
    ex = cx + 2 * LEAD
    ey = cy + 8
    gx, gy, gz = lax.axis_index("gx"), lax.axis_index("gy"), lax.axis_index("gz")
    me = (gx * ny + gy) * nz + gz
    f32 = jnp.float32

    def coords(t):
        return {"gx": t // (ny * nz), "gy": (t // nz) % ny, "gz": t % nz}

    lane = lax.broadcasted_iota(jnp.int32, (ey, 128), 1)
    row8 = lax.broadcasted_iota(jnp.int32, (8, 128), 0)
    rows = lax.broadcasted_iota(jnp.int32, (ey, 128), 0)
    lane1 = lax.broadcasted_iota(jnp.int32, (1, 128), 1)

    load = pltpu.make_async_copy(defl_hbm, defl, d_local)
    load.start()
    for ref in (
        zext.at[0], zext.at[1], got_low.at[0], got_low.at[1], got_high.at[0], got_high.at[1],
        cor, mext, got_low_c, got_high_c, got_low_m, got_high_m,
    ):
        lead = ref.shape[0]
        for c in range(lead):
            def clear(i, _, ref=ref, c=c):
                ref[c, i] = jnp.zeros(ref.shape[2:], f32)
                return 0
            lax.fori_loop(0, ref.shape[1], clear, 0)
    zgot[...] = jnp.zeros(zgot.shape, f32)

    barrier = pltpu.get_barrier_semaphore()

    def greet(j, _):
        t = lax.rem(me + j, n)
        pl.semaphore_signal(barrier, inc=1, device_id=coords(t), device_id_type=MESH)
        return 0

    lax.fori_loop(1, n, greet, 0)
    pl.semaphore_wait(barrier, n - 1)

    slab = order // nz

    def slab_copy(j):
        t = lax.rem(gz + j, nz)
        return pltpu.make_async_remote_copy(
            src_ref=factor,
            dst_ref=full.at[gz],
            send_sem=f_send.at[j - 1],
            recv_sem=f_recv.at[j - 1],
            device_id={"gx": gx, "gy": gy, "gz": t},
            device_id_type=MESH,
        )

    for j in range(1, nz):
        slab_copy(j).start()
    own_slab = pltpu.make_async_copy(factor, full.at[gz], f_local)
    own_slab.start()

    def exists(dx, dy):
        ok = jnp.bool_(True)
        if dx < 0:
            ok = jnp.logical_and(ok, gx > 0)
        if dx > 0:
            ok = jnp.logical_and(ok, gx < nx - 1)
        if dy < 0:
            ok = jnp.logical_and(ok, gy > 0)
        if dy > 0:
            ok = jnp.logical_and(ok, gy < ny - 1)
        return ok

    def pieces(ext, lo, hi, glo, ghi, send, recv):
        half = cx // 2
        out = []
        for d, (dx, dy) in enumerate(DIRS):
            if dy == 0:
                src = ext.at[:, pl.ds(LEAD if dx < 0 else LEAD + cx - W, W), pl.ds(0, cy)]
                dst = ext.at[:, pl.ds(LEAD + cx if dx < 0 else LEAD - W, W), pl.ds(0, cy)]
            else:
                start, count = {0: (0, half), -1: (0, 2), 1: (half - 2, 2)}[dx]
                to = {0: 2, -1: 2 + half, 1: 0}[dx]
                src = (lo if dy < 0 else hi).at[:, pl.ds(start, count)]
                dst = (glo if dy < 0 else ghi).at[:, pl.ds(to, count)]
            copy = pltpu.make_async_remote_copy(
                src_ref=src,
                dst_ref=dst,
                send_sem=send.at[d],
                recv_sem=recv.at[d],
                device_id={"gx": gx + dx, "gy": gy + dy, "gz": gz},
                device_id_type=MESH,
            )
            out.append((dx, dy, copy))
        return out

    def send_halo(ext, lo, hi, glo, ghi, send, recv):
        def pack(i, _):
            for c in range(ext.shape[0]):
                even, odd = LEAD + 2 * i, LEAD + 2 * i + 1
                lo[c, i] = jnp.where(row8 < 4, ext[c, even, 0:8], pltpu.roll(ext[c, odd, 0:8], 4, 0))
                hi[c, i] = jnp.where(
                    row8 >= 4, ext[c, even, cy - 8 : cy], pltpu.roll(ext[c, odd, cy - 8 : cy], 4, 0)
                )
            return 0

        lax.fori_loop(0, cx // 2, pack, 0)
        for dx, dy, copy in pieces(ext, lo, hi, glo, ghi, send, recv):
            pl.when(exists(dx, dy))(copy.start)

    def take_halo(ext, lo, hi, glo, ghi, send, recv):
        for dx, dy, copy in pieces(ext, lo, hi, glo, ghi, send, recv):
            pl.when(exists(-dx, -dy))(copy.wait_recv)
            pl.when(exists(dx, dy))(copy.wait_send)

        def unpack(i, _):
            for c in range(ext.shape[0]):
                a, b = glo[c, i], ghi[c, i]
                ext[c, 2 * i, cy : cy + 8] = jnp.where(row8 < 4, a, b)
                ext[c, 2 * i + 1, cy : cy + 8] = jnp.where(
                    row8 < 4, pltpu.roll(a, 4, 0), pltpu.roll(b, 4, 0)
                )
            return 0

        lax.fori_loop(0, ex // 2, unpack, 0)

    def halo_z(slot):
        return (
            zext.at[slot], low, high, got_low.at[slot], got_high.at[slot],
            zx_send, zx_recv.at[slot],
        )

    halo_m = (mext, low_m, high_m, got_low_m, got_high_m, m_send, m_recv)

    eighth = cx // 8

    def thin_pieces():
        out = []
        for d, (dx, dy) in enumerate(DIRS):
            if dy == 0:
                src = cor.at[:, pl.ds(LEAD if dx < 0 else LEAD + cx - 1, 1), pl.ds(0, cy)]
                dst = cor.at[:, pl.ds(LEAD + cx if dx < 0 else LEAD - 1, 1), pl.ds(0, cy)]
            else:
                start, count = {0: (0, eighth), -1: (0, 1), 1: (eighth - 1, 1)}[dx]
                to = {0: 1, -1: 1 + eighth, 1: 0}[dx]
                src = (low_c if dy < 0 else high_c).at[:, pl.ds(start, count)]
                dst = (got_low_c if dy < 0 else got_high_c).at[:, pl.ds(to, count)]
            copy = pltpu.make_async_remote_copy(
                src_ref=src,
                dst_ref=dst,
                send_sem=c_send.at[d],
                recv_sem=c_recv.at[d],
                device_id={"gx": gx + dx, "gy": gy + dy, "gz": gz},
                device_id_type=MESH,
            )
            out.append((dx, dy, copy))
        return out

    def send_thin():
        for c in range(3):
            for t in range(eighth):
                lo = hi = jnp.zeros((8, 128), f32)
                for j in range(8):
                    x = LEAD + 8 * t + j
                    lo = jnp.where(row8 == j, pltpu.roll(cor[c, x, 0:8], j, 0) if j else cor[c, x, 0:8], lo)
                    a = cor[c, x, cy - 8 : cy]
                    hi = jnp.where(row8 == j, pltpu.roll(a, (j + 1) % 8, 0) if j < 7 else a, hi)
                low_c[c, t] = lo
                high_c[c, t] = hi
        for dx, dy, copy in thin_pieces():
            pl.when(exists(dx, dy))(copy.start)

    def take_thin():
        for dx, dy, copy in thin_pieces():
            pl.when(exists(-dx, -dy))(copy.wait_recv)
            pl.when(exists(dx, dy))(copy.wait_send)
        for c in range(3):
            for t in range(eighth + 2):
                a, b = got_low_c[c, t], got_high_c[c, t]
                for j in range(8):
                    x = LEAD - 8 + 8 * t + j
                    if LEAD - 1 <= x <= LEAD + cx:
                        p = pltpu.roll(a, 8 - j, 0) if j else a
                        q = pltpu.roll(b, 7 - j, 0) if j < 7 else b
                        cor[c, x, cy : cy + 8] = jnp.where(row8 < 4, p, q)

    def columns(stage, side):
        return pltpu.make_async_remote_copy(
            src_ref=zsend.at[stage, side],
            dst_ref=zgot.at[stage, 1 - side],
            send_sem=zc_send.at[stage, side],
            recv_sem=zc_recv.at[stage, side],
            device_id={"gx": gx, "gy": gy, "gz": gz + (2 * side - 1)},
            device_id_type=MESH,
        )

    has = (gz > 0, gz < nz - 1)

    def send_columns(u, stage, first, last):
        for side in (0, 1):
            @pl.when(has[side])
            def _(side=side):
                def gather(x, acc):
                    shift = x if side == 0 else x + 1
                    return tuple(
                        jnp.where(lane == x, pltpu.roll(u[c, x], shift, 1), acc[c]) for c in range(3)
                    )

                acc = lax.fori_loop(first, last, gather, (jnp.zeros((ey, 128), f32),) * 3, unroll=2)
                for c in range(3):
                    zsend[stage, side, c] = acc[c]
                columns(stage, side).start()

    def take_columns(stage):
        for side in (0, 1):
            pl.when(has[1 - side])(columns(stage, side).wait_recv)
            pl.when(has[side])(columns(stage, side).wait_send)
        for side in (0, 1):
            bx, by = zgot[stage, side, 0], zgot[stage, side, 1]
            vzb[side] = (
                pltpu.roll(bx, 127, 1) - pltpu.roll(bx, 1, 1)
                + pltpu.roll(by, ey - 1, 0) - pltpu.roll(by, 1, 0)
            )

    def exchange_columns(u, stage, first, last):
        send_columns(u, stage, first, last)
        take_columns(stage)

    def y_pair(v):
        return pltpu.roll(v, ey - 1, 0), pltpu.roll(v, 1, 0)

    def z_pair(v, upper, lower, x):
        up = jnp.where(lane == 127, pltpu.roll(upper, 127 - x, 1), pltpu.roll(v, 127, 1))
        down = jnp.where(lane == 0, pltpu.roll(lower, 128 - x, 1), pltpu.roll(v, 1, 1))
        return up, down

    def off_diagonal(u, stage, first, last, use, carry):
        def before(x, _):
            p, m = y_pair(u[1, x])
            q, r = z_pair(u[2, x], zgot[stage, 1, 2], zgot[stage, 0, 2], x)
            vx[x] = (p - m) + (q - r)
            return 0

        lax.fori_loop(first - 1, last + 1, before, 0, unroll=2)

        def at(x, carry):
            pair, diff = [], []
            for c in range(3):
                v = u[c, x]
                xp, xm = u[c, x + 1], u[c, x - 1]
                yp, ym = y_pair(v)
                zp, zm = z_pair(v, zgot[stage, 1, c], zgot[stage, 0, c], x)
                pair.append((xp + xm, yp + ym, zp + zm))
                diff.append(((xp - xm), (yp - ym), (zp - zm))[c])
            px, py, pz = diff
            dx = vx[x + 1] - vx[x - 1]
            yp, ym = y_pair(px + pz)
            zp, zm = z_pair(px + py, vzb[1], vzb[0], x)
            mixed = (dx, yp - ym, zp - zm)
            off = tuple(
                0.25 * (pair[c][0] + pair[c][1] + pair[c][2]) + 0.625 * pair[c][c] + 0.15625 * mixed[c]
                for c in range(3)
            )
            return use(x, off, carry)

        return lax.fori_loop(first, last, at, carry)

    base = lax.rem(me, 8) * vectors if vectors * 8 == 128 else 0

    def share(slot, gamma, energy):
        def part(x, acc):
            acc = list(acc)
            for c in range(3):
                v = zext[slot, c, LEAD + x, 0:cy]
                for k in range(vectors):
                    prod = defl[k, c, x] * v
                    for t in range(0, cy, 8):
                        acc[k] = acc[k] + prod[t : t + 8]
            return tuple(acc)

        acc = lax.fori_loop(0, cx, part, (jnp.zeros((8, 128), f32),) * vectors)
        line = jnp.zeros((1, 128), f32)
        for k in range(vectors):
            total = jnp.sum(jnp.sum(acc[k], axis=0, keepdims=True), axis=1, keepdims=True)
            line = jnp.where(lane1 == base + k, total, line)
        gsend[slot, 0:1] = line
        gsend[slot, 1:2] = jnp.where(lane1 == 0, gamma, jnp.where(lane1 == 1, energy, 0.0))
        gat[slot, me] = gsend[slot]

        def push(j, _):
            t = lax.rem(me + j, n)
            pltpu.make_async_remote_copy(
                src_ref=gsend.at[slot],
                dst_ref=gat.at[slot, me],
                send_sem=g_send.at[slot],
                recv_sem=g_recv.at[slot, me],
                device_id=coords(t),
                device_id_type=MESH,
            ).start()
            return 0

        lax.fori_loop(1, n, push, 0)

    def collect(slot):
        def await_one(j, _):
            t = lax.rem(me + j, n)
            pltpu.make_async_copy(gsend.at[slot], gat.at[slot, t], g_recv.at[slot, t]).wait()
            return 0

        lax.fori_loop(1, n, await_one, 0)
        pltpu.make_async_copy(
            gat.at[slot, pl.ds(0, n - 1)], gat.at[slot, pl.ds(0, n - 1)], g_send.at[slot]
        ).wait()
        lines, scal = [], jnp.zeros((1, 128), f32)
        for t in range(n // 8):
            both = jnp.zeros((2, 128), f32)
            for s in range(8):
                both = both + gat[slot, 8 * t + s]
            lines.append(both[0:1])
            scal = scal + both[1:2]
        gamma = jnp.sum(jnp.where(lane1 == 0, scal, 0.0), axis=1, keepdims=True)
        energy = jnp.sum(jnp.where(lane1 == 1, scal, 0.0), axis=1, keepdims=True)
        return lines, gamma, energy

    def fill(x, _):
        for c in range(3):
            zext[0, c, LEAD + x, 0:cy] = forces[c, x]
            sol[c, x] = jnp.zeros((cy, 128), f32)
            direc[c, x] = jnp.zeros((cy, 128), f32)
        mext[0, LEAD + x, 0:cy] = mass[x]
        return 0

    lax.fori_loop(0, cx, fill, 0)
    send_halo(*halo_z(0))
    send_halo(*halo_m)
    load.wait()
    zero = jnp.zeros((1, 1), f32)
    share(0, zero, zero)

    for j in range(1, nz):
        copy = slab_copy(j)
        copy.wait_recv()
        copy.wait_send()
    own_slab.wait()
    per_slab = slab // BLOCK
    blocks = order // BLOCK
    group = min(4, blocks)
    r_i = lax.broadcasted_iota(jnp.int32, (BLOCK, BLOCK), 0)
    c_i = lax.broadcasted_iota(jnp.int32, (BLOCK, BLOCK), 1)

    def invert(g, _):
        lows, xs = [], []
        for q in range(group):
            i = g * group + q
            at = pl.ds(pl.multiple_of((i % per_slab) * BLOCK, BLOCK), BLOCK)
            col = pl.ds(pl.multiple_of(i * BLOCK, BLOCK), BLOCK)
            block = full[i // per_slab, at, col]
            lows.append(block)
            xs.append(jnp.where(r_i == c_i, 1.0 / jnp.where(r_i == c_i, block, 1.0), 0.0))
        s = 1
        while s < BLOCK:
            pick = (r_i // (2 * s) == c_i // (2 * s)) & ((r_i // s) % 2 == 1) & ((c_i // s) % 2 == 0)
            mids = [dot(jnp.where(pick, lows[q], 0.0), xs[q]) for q in range(group)]
            xs = [xs[q] - dot(xs[q], mids[q]) for q in range(group)]
            s *= 2
        for q in range(group):
            inv[g * group + q] = xs[q]
        return 0

    lax.fori_loop(0, blocks // group, invert, 0)

    width = min(512, order)

    def wipe(i, _):
        sol_mat[pl.ds(pl.multiple_of(i * 8, 8), 8), :] = jnp.zeros((8, order), f32)
        return 0

    lax.fori_loop(0, order // 8, wipe, 0)
    w_rows = lax.broadcasted_iota(jnp.int32, (BLOCK, width), 0)

    def substitute(i, _):
        at = pl.ds(pl.multiple_of((i % per_slab) * BLOCK, BLOCK), BLOCK)

        def over(j, _):
            col = pl.ds(pl.multiple_of(j * width, width), width)
            right = jnp.where(w_rows + i * BLOCK == slot_column[:, col], 1.0, 0.0)
            right = right - dot(full[i // per_slab, at, :], sol_mat[:, col])
            sol_mat[pl.ds(pl.multiple_of(i * BLOCK, BLOCK), BLOCK), col] = dot(inv[i], right)
            return 0

        lax.fori_loop(0, order // width, over, 0)
        return 0

    lax.fori_loop(0, blocks, substitute, 0)

    lines, _, _ = collect(0)
    for t in range(n // 8):
        gres[t] = lines[t]
        gdir[t] = jnp.zeros((1, 128), f32)

    strip = 64

    def coarse():
        own = pl.ds(pl.multiple_of((me // 8) * 128, 128), 128)

        def some(i, acc):
            at = pl.ds(pl.multiple_of(i * strip, strip), strip)
            y = jnp.zeros((strip, 128), f32)
            for t in range(order // 128):
                y = y + sol_mat[at, t * 128 : (t + 1) * 128] * gres[t]
            y = jnp.sum(y, axis=1, keepdims=True)
            return acc + jnp.sum(y * sol_mat[at, own], axis=0, keepdims=True)

        line = lax.fori_loop(0, order // strip, some, jnp.zeros((1, 128), f32), unroll=2)
        weights = [
            jnp.sum(jnp.where(lane1 == base + k, line, 0.0), axis=1, keepdims=True)
            for k in range(vectors)
        ]
        spread = [jnp.broadcast_to(w, (8, 128)) for w in weights]

        def correct(x, _):
            for c in range(3):
                for t in range(0, cy, 8):
                    acc = spread[0] * defl[0, c, x, t : t + 8]
                    for k in range(1, vectors):
                        acc = acc + spread[k] * defl[k, c, x, t : t + 8]
                    cor[c, LEAD + x, t : t + 8] = acc
            return 0

        lax.fori_loop(0, cx, correct, 0)

    coarse()
    send_thin()
    take_halo(*halo_z(0))
    take_halo(*halo_m)
    y_ok = (rows < cy) | ((rows < cy + 4) & (gy < ny - 1)) | ((rows >= cy + 4) & (gy > 0))

    def settle(x, _):
        x_ok = ((x >= LEAD) | (gx > 0)) & ((x < LEAD + cx) | (gx < nx - 1))
        keep = jnp.where(x_ok, 1.0, 0.0)
        cext[x] = jnp.where(y_ok, 0.6 / (mext[0, x] + 2.75), 0.0) * keep
        for c in range(3):
            rext[c, x] = zext[0, c, x]
            idir[c, x] = jnp.zeros((ey, 128), f32)
        return 0

    lax.fori_loop(0, ex, settle, 0)

    def iterate(it, carry):
        gamma_prior, step_prior = carry
        slot = lax.rem(it + 1, 2)
        def start(x, _):
            for c in range(3):
                ua[c, x] = cext[x] * rext[c, x]
            return 0

        lax.fori_loop(LEAD - 3, LEAD + cx + 3, start, 0)

        def sweep(src, dst):
            def use(x, off, carry):
                for c in range(3):
                    dst[c, x] = 0.4 * src[c, x] + cext[x] * (rext[c, x] + off[c])
                return carry
            return use

        exchange_columns(ua, 0, LEAD - 3, LEAD + cx + 3)
        off_diagonal(ua, 0, LEAD - 2, LEAD + cx + 2, sweep(ua, ub), 0)
        exchange_columns(ub, 1, LEAD - 2, LEAD + cx + 2)
        off_diagonal(ub, 1, LEAD - 1, LEAD + cx + 1, sweep(ub, uz), 0)
        take_thin()

        def join(x, _):
            for c in range(3):
                uz[c, x] = uz[c, x] + cor[c, x]
            return 0

        lax.fori_loop(LEAD - 1, LEAD + cx + 1, join, 0)
        exchange_columns(uz, 2, LEAD - 1, LEAD + cx + 1)

        def image(x, off, carry):
            gam, ene = carry
            diag = mext[0, x, 0:cy] + 2.75
            for c in range(3):
                z = uz[c, x, 0:cy]
                a = diag * z - off[c][0:cy]
                zext[slot, c, x, 0:cy] = a
                gam = gam + rext[c, x, 0:cy] * z
                ene = ene + z * a
            return gam, ene

        nothing = jnp.zeros((cy, 128), f32)
        gam, ene = off_diagonal(uz, 2, LEAD, LEAD + cx, image, (nothing, nothing))
        gam = jnp.sum(jnp.sum(gam, axis=0, keepdims=True), axis=1, keepdims=True)
        ene = jnp.sum(jnp.sum(ene, axis=0, keepdims=True), axis=1, keepdims=True)

        @pl.when(it < ITERS - 1)
        def _():
            send_halo(*halo_z(slot))

        share(slot, gam, ene)
        lines, gamma, energy = collect(slot)
        momentum = jnp.where(it == 0, 0.0, gamma / gamma_prior)
        step = gamma / (energy - momentum * gamma / step_prior)

        for t in range(n // 8):
            image_line = lines[t] + momentum * gdir[t]
            gdir[t] = image_line
            gres[t] = gres[t] - step * image_line

        @pl.when(it < ITERS - 1)
        def _():
            coarse()
            send_thin()

        def advance(x, _):
            for c in range(3):
                d = uz[c, LEAD + x, 0:cy] + momentum * direc[c, x]
                direc[c, x] = d
                sol[c, x] = sol[c, x] + step * d
            return 0

        lax.fori_loop(0, cx, advance, 0)

        @pl.when(it < ITERS - 1)
        def _():
            take_halo(*halo_z(slot))

        def update(x, _):
            for c in range(3):
                image_dir = zext[slot, c, x] + momentum * idir[c, x]
                idir[c, x] = image_dir
                rext[c, x] = rext[c, x] - step * image_dir
            return 0

        lax.fori_loop(LEAD - 3, LEAD + cx + 3, update, 0)
        return gamma, step

    one = jnp.ones((1, 1), f32)
    lax.fori_loop(0, ITERS, iterate, (one, one))

    def give(x, _):
        for c in range(3):
            res[c, x] = rext[c, LEAD + x, 0:cy]
        return 0

    lax.fori_loop(0, cx, give, 0)


def solution(mesh):
    nx, ny, nz = mesh.shape["gx"], mesh.shape["gy"], mesh.shape["gz"]

    def body(forces, mass_shift, deflation, coarse_factor, coarse_slot):
        vectors = deflation.shape[0]
        cx, cy = forces.shape[1], forces.shape[2]
        order = coarse_factor.shape[1]
        slab = coarse_factor.shape[0]
        n = nx * ny * nz
        slot_column = (
            coarse_slot[:, None] * vectors + jnp.arange(vectors, dtype=jnp.int32)[None, :]
        ).reshape(1, -1)
        ex, ey = cx + 2 * LEAD, cy + 8
        f32 = jnp.float32
        vm = lambda *shape: pltpu.VMEM(shape, f32)
        packs = lambda c: [
            vm(c, cx // 2, 8, 128), vm(c, cx // 2, 8, 128),
            vm(c, ex // 2, 8, 128), vm(c, ex // 2, 8, 128),
        ]
        field = (3, ex, ey, 128)
        dma = pltpu.SemaphoreType.DMA
        return pl.pallas_call(
            functools.partial(kernel, (nx, ny, nz, cx, cy, vectors, order)),
            out_shape=[jax.ShapeDtypeStruct(forces.shape, f32)] * 3,
            in_specs=[
                pl.BlockSpec(memory_space=pl.ANY if i == 2 else pltpu.VMEM) for i in range(5)
            ],
            out_specs=[pl.BlockSpec(memory_space=pltpu.VMEM)] * 3,
            scratch_shapes=[
                vm(2, *field), vm(*field), vm(*field), vm(ex, ey, 128), vm(1, ex, ey, 128),
                vm(*field), vm(*field), vm(*field), vm(*field), vm(ex, ey, 128),
                vm(3, cx // 2, 8, 128), vm(3, cx // 2, 8, 128),
                vm(2, 3, ex // 2, 8, 128), vm(2, 3, ex // 2, 8, 128),
                vm(3, cx // 8, 8, 128), vm(3, cx // 8, 8, 128),
                vm(3, cx // 8 + 2, 8, 128), vm(3, cx // 8 + 2, 8, 128),
                *packs(1),
                vm(3, 2, 3, ey, 128), vm(3, 2, 3, ey, 128), vm(2, ey, 128), vm(*deflation.shape),
                vm(nz, slab, order), vm(order // BLOCK, BLOCK, BLOCK), vm(order, order),
                vm(2, 2, 128), vm(2, n, 2, 128), vm(n // 8, 1, 128), vm(n // 8, 1, 128),
                dma((8,)), dma((2, 8)), dma((8,)), dma((8,)), dma((8,)), dma((8,)),
                dma((3, 2)), dma((3, 2)), dma((2,)), dma((2, n)),
                dma((max(nz - 1, 1),)), dma((max(nz - 1, 1),)), dma, dma,
            ],
            compiler_params=pltpu.CompilerParams(
                collective_id=0, has_side_effects=True, vmem_limit_bytes=66 * 1000 * 1000
            ),
        )(forces, mass_shift, deflation, coarse_factor, slot_column)

    return jax.shard_map(
        body,
        mesh=mesh,
        in_specs=(
            P(None, "gx", "gy", "gz"),
            P("gx", "gy", "gz"),
            P(None, None, "gx", "gy", "gz"),
            P("gz", None),
            P(),
        ),
        out_specs=(P(None, "gx", "gy", "gz"), P(None, "gx", "gy", "gz"), P(None, "gx", "gy", "gz")),
        check_vma=False,
    )
```

profile of v0, /device:TPU:0, one launch (start us, length us, event | category | flops | bytes accessed | tf_op | source)
XLA Modules:
  0.0 132.8 jit_solution(10986009970259132117)
XLA Ops:
  0.6 0.7 broadcast_multiply_fusion
  1.3 0.1 iota_add_fusion
  1.4 0.7 add.26.slot_column
  2.0 125.5 %shard_map.76 = (f32[3,16,16,128]{3,2,1,0:T(8,128)}, f32[3,16,16,128]{3,2,1,0:T(8,128)}, f32[3,16,16,128]{3,2,1,0:T(8,128)}) custom-call(f32[3,16,16,128]{3,2,1,0:T(8,128)} %forces.1, f32[16,16,128]{2,1,0:T(8,128)} %mass.1, f32[16,3,16,16,128]{4,3,2,1,0:T(8,128)} %defl_hbm.1, f32[256,512]{1,0:T(8,128)} %factor.1, s32[1,512]{1,0:T(1,128)} %add.26.slot_column), custom_call_target="tpu_custom_call" | custom-call | tf_op jit(solution)/shard_map/pallas_call | solution.py:603
  127.5 1.8 %copy.11 = f32[3,16,16,128]{3,2,1,0:T(8,128)} copy(f32[3,16,16,128]{3,2,1,0:T(8,128)} %get-tuple-element.6) | data formatting | bytes 786432
  129.3 1.8 %copy.12 = f32[3,16,16,128]{3,2,1,0:T(8,128)} copy(f32[3,16,16,128]{3,2,1,0:T(8,128)} %get-tuple-element.7) | data formatting | bytes 786432
  131.1 1.8 %copy.13 = f32[3,16,16,128]{3,2,1,0:T(8,128)} copy(f32[3,16,16,128]{3,2,1,0:T(8,128)} %get-tuple-element.8) | data formatting | bytes 786432
where the time goes:
time: 133 us
  Pallas kernels  126 us (95%)
  local copies, waits for them, and re-layouts  5.96 us (4%)
    pallas_call x1, Pallas kernels, body(): pl.pallas_call(functools.partial(kernel, (nx, ny, nz, cx, cy, vectors, or...  126 us
    unnamed x3, local copies, waits for them, and re-layouts  5.3 us

commit v1 on v0

v1 whole, which is shorter than its diff:
```python
import functools

import jax
import jax.numpy as jnp
from jax import lax
from jax.experimental import pallas as pl
from jax.experimental.pallas import tpu as pltpu
from jax.sharding import PartitionSpec as P

SWEEPS = 3
ITERS = 4
MESH = pl.DeviceIdType.MESH
HIGHEST = lax.Precision.HIGHEST
W = SWEEPS
DIRS = ((0, -1), (0, 1), (-1, 0), (1, 0), (-1, -1), (-1, 1), (1, -1), (1, 1))
BLOCK = 128


def dot(a, b):
    return jnp.dot(a, b, precision=HIGHEST, preferred_element_type=jnp.float32)


def up8(v):
    return -(-v // 8) * 8


def kernel(
    sizes,
    forces, mass, defl_hbm, factor, slots_hbm,
    sol, res, direc,
    zext, rext, idir, cext, cquarter, mext, cor, ua, ub, uz,
    zsend, zgot, edge, fix, cpack, defl,
    full, inv, sol_mat, turned, krows, gsend, gat, gres, gdir, slots,
    zx_send, zx_recv, c_send, c_recv, m_send, m_recv,
    zc_send, zc_recv, g_send, g_recv, f_send, f_recv, i_send, i_recv, local,
):
    nx, ny, nz, cx, cy, vectors, order = sizes
    n = nx * ny * nz
    ex = cx + 2 * W
    pitch = zext.shape[3]
    tall = up8(cy + 2 * W)
    gx, gy, gz = lax.axis_index("gx"), lax.axis_index("gy"), lax.axis_index("gz")
    me = (gx * ny + gy) * nz + gz
    f32 = jnp.float32

    def wrap(a, d, size):
        s = a + d
        return jnp.where(s >= size, s - size, s)

    others = [
        {"gx": wrap(gx, dx, nx), "gy": wrap(gy, dy, ny), "gz": wrap(gz, dz, nz)}
        for dx in range(nx) for dy in range(ny) for dz in range(nz) if (dx, dy, dz) != (0, 0, 0)
    ]
    own_x, own_y = pl.ds(W, cx), pl.ds(W, cy)
    load_factor = pltpu.make_async_copy(factor, full.at[gz], local.at[0])
    load_factor.start()
    load_slots = pltpu.make_async_copy(slots_hbm, slots, local.at[1])
    load_slots.start()

    def clear(ref):
        lead = ref.shape[0]
        zero = jnp.zeros(ref.shape[2:], f32)

        def one(i, _):
            for c in range(lead):
                ref[c, i] = zero
            return 0

        lax.fori_loop(0, ref.shape[1], one, 0)

    for ref in (zext.at[0], zext.at[1], mext, cor):
        clear(ref)
    zgot[...] = jnp.zeros(zgot.shape, f32)
    barrier = pltpu.get_barrier_semaphore()
    for other in others:
        pl.semaphore_signal(barrier, inc=1, device_id=other, device_id_type=MESH)
    load_forces = pltpu.make_async_copy(forces, zext.at[0, :, own_x, own_y], local.at[2])
    load_forces.start()
    load_mass = pltpu.make_async_copy(mass, mext.at[0, own_x, own_y], local.at[3])
    load_mass.start()
    load_defl = pltpu.make_async_copy(defl_hbm, defl, local.at[4])
    load_defl.start()
    for ref in (ua, ub, uz):
        clear(ref)
    for ref in (zsend, edge, fix, cpack):
        ref[...] = jnp.zeros(ref.shape, f32)

    lane = lax.broadcasted_iota(jnp.int32, (tall, 128), 1)
    lane8 = lax.broadcasted_iota(jnp.int32, (8, 128), 1)
    row8 = lax.broadcasted_iota(jnp.int32, (8, 128), 0)
    lane1 = lax.broadcasted_iota(jnp.int32, (1, 128), 1)
    rim = (lane == 0) | (lane == 127)
    rim_own = (lax.broadcasted_iota(jnp.int32, (cy, 128), 1) + 1) % 128 < 2
    even = lane % 2 == 0
    sign = jnp.where(even, 0.15625, -0.15625)
    base = (me % 8) * vectors

    slab = order // nz
    per_slab = slab // BLOCK
    blocks = order // BLOCK
    r_i = lax.broadcasted_iota(jnp.int32, (BLOCK, BLOCK), 0)
    c_i = lax.broadcasted_iota(jnp.int32, (BLOCK, BLOCK), 1)
    load_factor.wait()
    lows, xs = [], []
    for q in range(per_slab):
        col = pl.ds(pl.multiple_of((gz * per_slab + q) * BLOCK, BLOCK), BLOCK)
        block = full[gz, q * BLOCK : (q + 1) * BLOCK, col]
        lows.append(block)
        xs.append(jnp.where(r_i == c_i, 1.0 / jnp.where(r_i == c_i, block, 1.0), 0.0))
    s = 1
    while s < BLOCK:
        pick = (r_i // (2 * s) == c_i // (2 * s)) & ((r_i // s) % 2 == 1) & ((c_i // s) % 2 == 0)
        mids = [dot(jnp.where(pick, lows[q], 0.0), xs[q]) for q in range(per_slab)]
        xs = [xs[q] - dot(xs[q], mids[q]) for q in range(per_slab)]
        s *= 2
    for q in range(per_slab):
        inv[gz * per_slab + q] = xs[q]

    def slab_copies(j):
        t = wrap(gz, j, nz)
        to = {"gx": gx, "gy": gy, "gz": t}
        mine = pl.ds(gz * per_slab, per_slab)
        return (
            pltpu.make_async_remote_copy(
                src_ref=full.at[gz], dst_ref=full.at[gz], send_sem=f_send.at[j - 1],
                recv_sem=f_recv.at[j - 1], device_id=to, device_id_type=MESH,
            ),
            pltpu.make_async_remote_copy(
                src_ref=inv.at[mine], dst_ref=inv.at[mine], send_sem=i_send.at[j - 1],
                recv_sem=i_recv.at[j - 1], device_id=to, device_id_type=MESH,
            ),
        )

    def exists(dx, dy):
        ok = jnp.bool_(True)
        if dx < 0:
            ok = jnp.logical_and(ok, gx > 0)
        if dx > 0:
            ok = jnp.logical_and(ok, gx < nx - 1)
        if dy < 0:
            ok = jnp.logical_and(ok, gy > 0)
        if dy > 0:
            ok = jnp.logical_and(ok, gy < ny - 1)
        return ok

    def span(d, size, width):
        if d == 0:
            return pl.ds(W, size), pl.ds(W, size)
        if d < 0:
            return pl.ds(W, width), pl.ds(W + size, width)
        return pl.ds(W + size - width, width), pl.ds(W - width, width)

    def pieces(ext, width, send, recv):
        out = []
        for d, (dx, dy) in enumerate(DIRS):
            sx, tx = span(dx, cx, width)
            sy, ty = span(dy, cy, width)
            copy = pltpu.make_async_remote_copy(
                src_ref=ext.at[:, sx, sy],
                dst_ref=ext.at[:, tx, ty],
                send_sem=send.at[d],
                recv_sem=recv.at[d],
                device_id={"gx": gx + dx, "gy": gy + dy, "gz": gz},
                device_id_type=MESH,
            )
            out.append((dx, dy, copy))
        return out

    def send_halo(*args):
        for dx, dy, copy in pieces(*args):
            pl.when(exists(dx, dy))(copy.start)

    def take_halo(*args):
        for dx, dy, copy in pieces(*args):
            pl.when(exists(-dx, -dy))(copy.wait_recv)
            pl.when(exists(dx, dy))(copy.wait_send)

    def halo_z(slot):
        return zext.at[slot], W, zx_send, zx_recv.at[slot]

    halo_m = (mext, W, m_send, m_recv)
    thin = (cor, 1, c_send, c_recv)

    has = (gz > 0, gz < nz - 1)

    def columns(stage, side):
        return pltpu.make_async_remote_copy(
            src_ref=zsend.at[stage],
            dst_ref=zgot.at[stage, 1 - side],
            send_sem=zc_send.at[stage, side],
            recv_sem=zc_recv.at[stage, side],
            device_id={"gx": gx, "gy": gy, "gz": gz + (2 * side - 1)},
            device_id_type=MESH,
        )

    def gathered(v, x, acc):
        return jnp.where(lane // 2 == x, pltpu.roll(v, 2 * x + 1, 1), acc)

    nothing = (jnp.zeros((tall, 128), f32),) * 3

    def send_columns(stage, first, acc):
        for c in range(3):
            swapped = jnp.where(even, pltpu.roll(acc[c], 127, 1), pltpu.roll(acc[c], 1, 1))
            zsend[stage, c, first : first + tall] = swapped
        for side in (0, 1):
            pl.when(has[side])(columns(stage, side).start)

    def take_columns(stage, first, scaled):
        for side in (0, 1):
            pl.when(has[1 - side])(columns(stage, side).wait_recv)
            pl.when(has[side])(columns(stage, side).wait_send)
        e = []
        for c in range(3):
            v = jnp.where(
                even, zgot[stage, 1, c, first - 1 : first - 1 + tall], zgot[stage, 0, c, first - 1 : first - 1 + tall]
            ) - zsend[stage, c, first - 1 : first - 1 + tall]
            edge[c, first - 1 : first - 1 + tall] = v

        def at(c, dy):
            return edge[c, first + dy : first + dy + tall]

        def along(v):
            return pltpu.roll(v, 126, 1) - pltpu.roll(v, 2, 1)

        ex_, ey_, ez_ = at(0, 0), at(1, 0), at(2, 0)
        fx = 0.25 * ex_ + sign * along(ez_)
        fy = 0.25 * ey_ + sign * (at(2, 1) - at(2, -1))
        fz = 0.875 * ez_ + sign * (along(ex_) + (at(1, 1) - at(1, -1)))
        for c, f in enumerate((fx, fy, fz)):
            fix[c, first : first + tall] = cpack[first : first + tall] * f if scaled else f

    def stencil(u, x, r):
        def at(c, dx, dy):
            return u[c, x + dx, r + dy : r + dy + 8]

        def z_diff(v):
            return pltpu.roll(v, 127, 1) - pltpu.roll(v, 1, 1)

        here = [at(c, 0, 0) for c in range(3)]
        xp, xm = [at(c, 1, 0) for c in range(3)], [at(c, -1, 0) for c in range(3)]
        yp, ym = [at(c, 0, 1) for c in range(3)], [at(c, 0, -1) for c in range(3)]
        sx = [xp[c] + xm[c] for c in range(3)]
        sy = [yp[c] + ym[c] for c in range(3)]
        sz = [pltpu.roll(here[c], 127, 1) + pltpu.roll(here[c], 1, 1) for c in range(3)]
        mx = (at(1, 1, 1) - at(1, 1, -1)) - (at(1, -1, 1) - at(1, -1, -1)) + z_diff(xp[2] - xm[2])
        my = (at(0, 1, 1) - at(0, -1, 1)) - (at(0, 1, -1) - at(0, -1, -1)) + z_diff(yp[2] - ym[2])
        mz = z_diff((xp[0] - xm[0]) + (yp[1] - ym[1]))
        t = (
            (sy[0] + sz[0]) + 3.5 * sx[0] + 0.625 * mx,
            (sx[1] + sz[1]) + 3.5 * sy[1] + 0.625 * my,
            (sx[2] + sy[2]) + 3.5 * sz[2] + 0.625 * mz,
        )
        return here, t

    def sweep(src, dst, depth):
        first = W - depth
        rows = up8(cy + 2 * depth)

        def at(x, _):
            for r in range(first, first + rows, 8):
                here, t = stencil(src, x, r)
                q = cquarter[x, r : r + 8]
                for c in range(3):
                    if src is ua:
                        dst[c, x, r : r + 8] = 1.4 * here[c] + q * t[c]
                    else:
                        dst[c, x, r : r + 8] = 0.4 * here[c] + (ua[c, x, r : r + 8] + q * t[c])
            return 0

        lax.fori_loop(first, W + cx + depth, at, 0)

    def mend(u, depth, extra):
        first = W - depth
        part = slice(first, first + tall)

        def at(x, acc):
            out = []
            for c in range(3):
                v = u[c, x, part] + jnp.where(rim, pltpu.roll(fix[c, part], 127 - 2 * x, 1), 0.0)
                if extra is not None:
                    v = v + extra[c, x, part]
                u[c, x, part] = v
                out.append(gathered(v, x, acc[c]))
            return tuple(out)

        return lax.fori_loop(first, W + cx + depth, at, nothing)

    def push(slot, acc, gamma, energy):
        line = jnp.zeros((1, 128), f32)
        for k in range(vectors):
            total = jnp.sum(jnp.sum(acc[k], axis=0, keepdims=True), axis=1, keepdims=True)
            line = jnp.where(lane1 == base + k, total, line)
        if gamma is not None:
            line = jnp.where(lane1 == (base + vectors) % 128, gamma, line)
            line = jnp.where(lane1 == (base + vectors + 1) % 128, energy, line)
        gsend[slot, 0:1] = line
        gat[slot, pl.ds(me, 1)] = line
        for other in others:
            pltpu.make_async_remote_copy(
                src_ref=gsend.at[slot, 0],
                dst_ref=gat.at[slot, me],
                send_sem=g_send.at[slot],
                recv_sem=g_recv.at[slot],
                device_id=other,
                device_id_type=MESH,
            ).start()

    def collect(slot):
        rest = gat.at[slot, pl.ds(0, n - 1)]
        pltpu.make_async_copy(rest, rest, g_recv.at[slot]).wait()
        pltpu.make_async_copy(rest, rest, g_send.at[slot]).wait()
        lines, both = [], jnp.zeros((8, 128), f32)
        for t in range(n // 8):
            tile = gat[slot, 8 * t : 8 * t + 8]
            lines.append(jnp.sum(jnp.where(lane8 // vectors == row8, tile, 0.0), axis=0, keepdims=True))
            both = both + tile
        g_at = (row8 * vectors + vectors) % 128
        gamma = jnp.sum(jnp.where(lane8 == g_at, both, 0.0), axis=0, keepdims=True)
        energy = jnp.sum(jnp.where(lane8 == g_at + 1, both, 0.0), axis=0, keepdims=True)
        return lines, jnp.sum(gamma, axis=1, keepdims=True), jnp.sum(energy, axis=1, keepdims=True)

    def restrict(x, values, acc):
        acc = list(acc)
        for c in range(3):
            for k in range(vectors):
                prod = defl[k, c, x] * values[c]
                for t in range(0, cy, 8):
                    acc[k] = acc[k] + prod[t : t + 8]
        return acc

    clean = (jnp.zeros((8, 128), f32),) * vectors
    load_forces.wait()
    load_defl.wait()

    def first_share(x, acc):
        return tuple(restrict(x, [zext[0, c, W + x, W : W + cy] for c in range(3)], acc))

    acc = lax.fori_loop(0, cx, first_share, clean)
    load_mass.wait()

    pl.semaphore_wait(barrier, n - 1)
    push(0, acc, None, None)
    for j in range(1, nz):
        for copy in slab_copies(j):
            copy.start()
    send_halo(*halo_z(0))
    send_halo(*halo_m)

    load_slots.wait()
    for j in range(1, nz):
        for copy in slab_copies(j):
            copy.wait_recv()
            copy.wait_send()

    width = min(512, order)
    w_rows = lax.broadcasted_iota(jnp.int32, (BLOCK, width), 0)

    def slot_line(t):
        line = jnp.zeros((1, 128), jnp.int32)
        for r in range(8):
            line = jnp.where(lane1 // vectors == r, slots[8 * t + r] * vectors + lane1 % vectors, line)
        return line

    def one_hot(i, j):
        line = jnp.concatenate([slot_line(j * (width // 128) + t) for t in range(width // 128)], axis=1)
        return jnp.where(w_rows + i * BLOCK == line, 1.0, 0.0)

    if blocks <= 4:
        for i in range(blocks):
            right = one_hot(i, 0)
            if i:
                at = slice((i % per_slab) * BLOCK, (i % per_slab + 1) * BLOCK)
                right = right - dot(full[i // per_slab, at, 0 : i * BLOCK], sol_mat[0 : i * BLOCK])
            sol_mat[i * BLOCK : (i + 1) * BLOCK] = dot(inv[i], right)
    else:
        def wipe(i, _):
            sol_mat[pl.ds(pl.multiple_of(i * 8, 8), 8), :] = jnp.zeros((8, order), f32)
            return 0

        lax.fori_loop(0, order // 8, wipe, 0)

        def substitute(i, _):
            at = pl.ds(pl.multiple_of((i % per_slab) * BLOCK, BLOCK), BLOCK)
            for j in range(order // width):
                col = slice(j * width, (j + 1) * width)
                right = one_hot(i, j) - dot(full[i // per_slab, at, :], sol_mat[:, col])
                sol_mat[pl.ds(pl.multiple_of(i * BLOCK, BLOCK), BLOCK), col] = dot(inv[i], right)
            return 0

        lax.fori_loop(0, blocks, substitute, 0)

    mine = pl.ds(pl.multiple_of((me // 8) * 128, 128), 128)

    def turn(i, _):
        at = pl.ds(pl.multiple_of(i * BLOCK, BLOCK), BLOCK)
        turned[:, at] = sol_mat[at, mine].T
        return 0

    lax.fori_loop(0, blocks, turn, 0)
    own_rows = pl.ds(pl.multiple_of(base, 8), vectors)

    def form(j, _):
        col = pl.ds(pl.multiple_of(j * width, width), width)
        krows[:, col] = dot(turned[own_rows, :], sol_mat[:, col])
        return 0

    lax.fori_loop(0, order // width, form, 0)

    def coarse():
        y = jnp.zeros((vectors, 128), f32)
        for t in range(order // 128):
            y = y + krows[:, t * 128 : (t + 1) * 128] * gres[t]
        y = jnp.broadcast_to(jnp.sum(y, axis=1, keepdims=True), (vectors, 128))
        spread = [jnp.broadcast_to(y[k : k + 1], (8, 128)) for k in range(vectors)]

        def correct(x, _):
            for c in range(3):
                for t in range(0, cy, 8):
                    acc = spread[0] * defl[0, c, x, t : t + 8]
                    for k in range(1, vectors):
                        acc = acc + spread[k] * defl[k, c, x, t : t + 8]
                    cor[c, W + x, W + t : W + t + 8] = acc
            return 0

        lax.fori_loop(0, cx, correct, 0)

    lines, _, _ = collect(0)
    for t in range(n // 8):
        gres[t] = lines[t]
        gdir[t] = jnp.zeros((1, 128), f32)
    coarse()
    send_halo(*thin)
    take_halo(*halo_z(0))
    take_halo(*halo_m)
    rows = lax.broadcasted_iota(jnp.int32, (pitch, 128), 0)
    y_ok = ((rows >= W) | (gy > 0)) & ((rows < W + cy) | (gy < ny - 1)) & (rows < cy + 2 * W)

    def settle(x, acc):
        x_ok = ((x >= W) | (gx > 0)) & ((x < W + cx) | (gx < nx - 1))
        keep = jnp.where(x_ok, 1.0, 0.0)
        v = jnp.where(y_ok, 0.6 / (mext[0, x] + 2.75), 0.0) * keep
        cext[x] = v
        cquarter[x] = 0.25 * v
        out = [gathered(v[0:tall], x, acc[3])]
        new = []
        for c in range(3):
            f = zext[0, c, x]
            rext[c, x] = f
            idir[c, x] = jnp.zeros((pitch, 128), f32)
            u = v[0:tall] * f[0:tall]
            ua[c, x, 0:tall] = u
            new.append(gathered(u, x, acc[c]))
        return tuple(new) + tuple(out)

    acc = lax.fori_loop(0, ex, settle, nothing + (nothing[0],))
    cpack[0:tall] = acc[3]
    send_columns(0, 0, acc[0:3])

    def own_clear(x, _):
        for c in range(3):
            sol[c, x] = jnp.zeros((cy, 128), f32)
            direc[c, x] = jnp.zeros((cy, 128), f32)
        return 0

    lax.fori_loop(0, cx, own_clear, 0)

    def iterate(it, carry):
        gamma_prior, step_prior = carry
        slot = (it + 1) % 2
        sweep(ua, ub, 2)
        take_columns(0, 1, True)
        acc = mend(ub, 2, None)
        send_columns(1, 1, acc)
        sweep(ub, uz, 1)
        take_columns(1, 2, True)
        take_halo(*thin)
        acc = mend(uz, 1, cor)
        send_columns(2, 2, acc)

        def image(x, _):
            for t in range(0, cy, 8):
                here, off = stencil(uz, x, W + t)
                diag = mext[0, x, W + t : W + t + 8] + 2.75
                for c in range(3):
                    zext[slot, c, x, W + t : W + t + 8] = diag * here[c] - 0.25 * off[c]
            return 0

        lax.fori_loop(W, W + cx, image, 0)
        take_columns(2, 3, False)

        def finish(x, carry):
            gam, ene, acc = carry[0], carry[1], carry[2:]
            values = []
            for c in range(3):
                f = pltpu.roll(fix[c, W : W + cy], 127 - 2 * W - 2 * x, 1)
                a = zext[slot, c, W + x, W : W + cy] - jnp.where(rim_own, f, 0.0)
                zext[slot, c, W + x, W : W + cy] = a
                z = uz[c, W + x, W : W + cy]
                gam = gam + rext[c, W + x, W : W + cy] * z
                ene = ene + z * a
                values.append(a)
            return (gam, ene) + tuple(restrict(x, values, acc))

        blank = jnp.zeros((cy, 128), f32)
        carry = lax.fori_loop(0, cx, finish, (blank, blank) + clean)
        gam = jnp.sum(jnp.sum(carry[0], axis=0, keepdims=True), axis=1, keepdims=True)
        ene = jnp.sum(jnp.sum(carry[1], axis=0, keepdims=True), axis=1, keepdims=True)
        push(slot, carry[2:], gam, ene)

        @pl.when(it < ITERS - 1)
        def _():
            send_halo(*halo_z(slot))

        lines, gamma, energy = collect(slot)
        momentum = jnp.where(it == 0, 0.0, gamma / gamma_prior)
        step = gamma / (energy - momentum * gamma / step_prior)

        @pl.when(it < ITERS - 1)
        def _():
            for t in range(n // 8):
                image_line = lines[t] + momentum * gdir[t]
                gdir[t] = image_line
                gres[t] = gres[t] - step * image_line
            coarse()
            send_halo(*thin)
            take_halo(*halo_z(slot))

            def update(x, acc):
                out = []
                for c in range(3):
                    image_dir = zext[slot, c, x, 0:tall] + momentum * idir[c, x, 0:tall]
                    idir[c, x, 0:tall] = image_dir
                    r = rext[c, x, 0:tall] - step * image_dir
                    rext[c, x, 0:tall] = r
                    u = cext[x, 0:tall] * r
                    ua[c, x, 0:tall] = u
                    out.append(gathered(u, x, acc[c]))
                return tuple(out)

            acc = lax.fori_loop(0, ex, update, nothing)
            send_columns(0, 0, acc)

        def advance(x, _):
            for c in range(3):
                d = uz[c, W + x, W : W + cy] + momentum * direc[c, x]
                direc[c, x] = d
                sol[c, x] = sol[c, x] + step * d
            return 0

        lax.fori_loop(0, cx, advance, 0)

        @pl.when(it == ITERS - 1)
        def _():
            def give(x, _):
                for c in range(3):
                    image_dir = zext[slot, c, W + x, W : W + cy] + momentum * idir[c, W + x, W : W + cy]
                    res[c, x] = rext[c, W + x, W : W + cy] - step * image_dir
                return 0

            lax.fori_loop(0, cx, give, 0)

        return gamma, step

    one = jnp.ones((1, 1), f32)
    lax.fori_loop(0, ITERS, iterate, (one, one))


def solution(mesh):
    nx, ny, nz = mesh.shape["gx"], mesh.shape["gy"], mesh.shape["gz"]

    def body(forces, mass_shift, deflation, coarse_factor, coarse_slot):
        vectors = deflation.shape[0]
        cx, cy = forces.shape[1], forces.shape[2]
        order = coarse_factor.shape[1]
        slab = coarse_factor.shape[0]
        n = nx * ny * nz
        ex, pitch = cx + 2 * W, up8(up8(cy + 2 * W) + W)
        f32 = jnp.float32
        vm = lambda *shape: pltpu.VMEM(shape, f32)
        field = (3, ex, pitch, 128)
        dma = pltpu.SemaphoreType.DMA
        peers = max(nz - 1, 1)
        return pl.pallas_call(
            functools.partial(kernel, (nx, ny, nz, cx, cy, vectors, order)),
            out_shape=[jax.ShapeDtypeStruct(forces.shape, f32)] * 3,
            in_specs=[pl.BlockSpec(memory_space=pl.ANY)] * 5,
            out_specs=[pl.BlockSpec(memory_space=pltpu.VMEM)] * 3,
            scratch_shapes=[
                vm(2, *field), vm(*field), vm(*field), vm(ex, pitch, 128), vm(ex, pitch, 128),
                vm(1, ex, pitch, 128), vm(*field), vm(*field), vm(*field), vm(*field),
                vm(3, 3, pitch, 128), vm(3, 2, 3, pitch, 128), vm(3, pitch, 128), vm(3, pitch, 128),
                vm(pitch, 128), vm(*deflation.shape),
                vm(nz, slab, order), vm(order // BLOCK, BLOCK, BLOCK), vm(order, order),
                vm(BLOCK, order), vm(vectors, order),
                vm(2, 8, 128), vm(2, n, 128), vm(n // 8, 1, 128), vm(n // 8, 1, 128),
                pltpu.SMEM(coarse_slot.shape, jnp.int32),
                dma((8,)), dma((2, 8)), dma((8,)), dma((8,)), dma((8,)), dma((8,)),
                dma((3, 2)), dma((3, 2)), dma((2,)), dma((2,)),
                dma((peers,)), dma((peers,)), dma((peers,)), dma((peers,)), dma((5,)),
            ],
            compiler_params=pltpu.CompilerParams(
                collective_id=0, has_side_effects=True, vmem_limit_bytes=66 * 1000 * 1000
            ),
        )(forces, mass_shift, deflation, coarse_factor, coarse_slot)

    return jax.shard_map(
        body,
        mesh=mesh,
        in_specs=(
            P(None, "gx", "gy", "gz"),
            P("gx", "gy", "gz"),
            P(None, None, "gx", "gy", "gz"),
            P("gz", None),
            P(),
        ),
        out_specs=(P(None, "gx", "gy", "gz"), P(None, "gx", "gy", "gz"), P(None, "gx", "gy", "gz")),
        check_vma=False,
    )
```

time: 133 us -> 111 us (0.83)
  Pallas kernels: 126 us -> 105 us
    pallas_call x1, Pallas kernels: 126 us -> 105 us  [body(): pl.pallas_call(functools.partial(kernel, (nx, ny, nz, cx, cy, vectors, or...]
where the time goes in v1:
time: 111 us
  Pallas kernels  105 us (95%)
  local copies, waits for them, and re-layouts  5.3 us (5%)
    pallas_call x1, Pallas kernels, body(): pl.pallas_call(functools.partial(kernel, (nx, ny, nz, cx, cy, vectors, or...  105 us
    unnamed x3, local copies, waits for them, and re-layouts  5.3 us

profile of v1, /device:TPU:0, one launch (start us, length us, event | category | flops | bytes accessed | tf_op | source)
XLA Modules:
  0.0 110.5 jit_solution(14826876975551700719)
XLA Ops:
  0.6 104.6 %shard_map.76 = (f32[3,16,16,128]{3,2,1,0:T(8,128)}, f32[3,16,16,128]{3,2,1,0:T(8,128)}, f32[3,16,16,128]{3,2,1,0:T(8,128)}) custom-call(f32[3,16,16,128]{3,2,1,0:T(8,128)} %forces.1, f32[16,16,128]{2,1,0:T(8,128)} %mass.1, f32[16,3,16,16,128]{4,3,2,1,0:T(8,128)} %defl_hbm.1, f32[256,512]{1,0:T(8,128)} %factor.1, s32[32]{0:T(128)} %slots_hbm.1), custom_call_target="tpu_custom_call" | custom-call | tf_op jit(solution)/shard_map/pallas_call | solution.py:583
  105.2 1.8 %copy.11 = f32[3,16,16,128]{3,2,1,0:T(8,128)} copy(f32[3,16,16,128]{3,2,1,0:T(8,128)} %get-tuple-element.6) | data formatting | bytes 786432
  107.0 1.8 %copy.12 = f32[3,16,16,128]{3,2,1,0:T(8,128)} copy(f32[3,16,16,128]{3,2,1,0:T(8,128)} %get-tuple-element.7) | data formatting | bytes 786432
  108.8 1.8 %copy.13 = f32[3,16,16,128]{3,2,1,0:T(8,128)} copy(f32[3,16,16,128]{3,2,1,0:T(8,128)} %get-tuple-element.8) | data formatting | bytes 786432

commit v2 on v1

--- a/solution.py
+++ b/solution.py
@@ -22,6 +22,18 @@
 
 def up8(v):
     return -(-v // 8) * 8
+
+
+def planes(first, last, body, carry, most):
+    count = last - first
+    step = max(d for d in range(1, most + 1) if count % d == 0)
+
+    def some(i, carry):
+        for j in range(step):
+            carry = body(first + i * step + j, carry)
+        return carry
+
+    return lax.fori_loop(0, count // step, some, carry)
 
 
 def kernel(
@@ -233,22 +245,22 @@
         def at(c, dx, dy):
             return u[c, x + dx, r + dy : r + dy + 8]
 
-        def z_diff(v):
-            return pltpu.roll(v, 127, 1) - pltpu.roll(v, 1, 1)
-
         here = [at(c, 0, 0) for c in range(3)]
         xp, xm = [at(c, 1, 0) for c in range(3)], [at(c, -1, 0) for c in range(3)]
         yp, ym = [at(c, 0, 1) for c in range(3)], [at(c, 0, -1) for c in range(3)]
-        sx = [xp[c] + xm[c] for c in range(3)]
-        sy = [yp[c] + ym[c] for c in range(3)]
-        sz = [pltpu.roll(here[c], 127, 1) + pltpu.roll(here[c], 1, 1) for c in range(3)]
-        mx = (at(1, 1, 1) - at(1, 1, -1)) - (at(1, -1, 1) - at(1, -1, -1)) + z_diff(xp[2] - xm[2])
-        my = (at(0, 1, 1) - at(0, -1, 1)) - (at(0, 1, -1) - at(0, -1, -1)) + z_diff(yp[2] - ym[2])
-        mz = z_diff((xp[0] - xm[0]) + (yp[1] - ym[1]))
+
+        def along_z(even_part, odd_part):
+            return pltpu.roll(even_part + odd_part, 127, 1) + pltpu.roll(even_part - odd_part, 1, 1)
+
+        zx = along_z(here[0], 0.625 * (xp[2] - xm[2]))
+        zy = along_z(here[1], 0.625 * (yp[2] - ym[2]))
+        zz = along_z(3.5 * here[2], 0.625 * ((xp[0] - xm[0]) + (yp[1] - ym[1])))
+        mx = (at(1, 1, 1) - at(1, 1, -1)) - (at(1, -1, 1) - at(1, -1, -1))
+        my = (at(0, 1, 1) - at(0, -1, 1)) - (at(0, 1, -1) - at(0, -1, -1))
         t = (
-            (sy[0] + sz[0]) + 3.5 * sx[0] + 0.625 * mx,
-            (sx[1] + sz[1]) + 3.5 * sy[1] + 0.625 * my,
-            (sx[2] + sy[2]) + 3.5 * sz[2] + 0.625 * mz,
+            (yp[0] + ym[0]) + 3.5 * (xp[0] + xm[0]) + 0.625 * mx + zx,
+            (xp[1] + xm[1]) + 3.5 * (yp[1] + ym[1]) + 0.625 * my + zy,
+            (xp[2] + xm[2]) + (yp[2] + ym[2]) + zz,
         )
         return here, t
 
@@ -267,7 +279,7 @@
                         dst[c, x, r : r + 8] = 0.4 * here[c] + (ua[c, x, r : r + 8] + q * t[c])
             return 0
 
-        lax.fori_loop(first, W + cx + depth, at, 0)
+        planes(first, W + cx + depth, at, 0, 5)
 
     def mend(u, depth, extra):
         first = W - depth
@@ -283,7 +295,7 @@
                 out.append(gathered(v, x, acc[c]))
             return tuple(out)
 
-        return lax.fori_loop(first, W + cx + depth, at, nothing)
+        return planes(first, W + cx + depth, at, nothing, 6)
 
     def push(slot, acc, gamma, energy):
         line = jnp.zeros((1, 128), f32)
@@ -452,7 +464,7 @@
             new.append(gathered(u, x, acc[c]))
         return tuple(new) + tuple(out)
 
-    acc = lax.fori_loop(0, ex, settle, nothing + (nothing[0],))
+    acc = planes(0, ex, settle, nothing + (nothing[0],), 2)
     cpack[0:tall] = acc[3]
     send_columns(0, 0, acc[0:3])
 
@@ -485,7 +497,7 @@
                     zext[slot, c, x, W + t : W + t + 8] = diag * here[c] - 0.25 * off[c]
             return 0
 
-        lax.fori_loop(W, W + cx, image, 0)
+        planes(W, W + cx, image, 0, 4)
         take_columns(2, 3, False)
 
         def finish(x, carry):
@@ -502,7 +514,7 @@
             return (gam, ene) + tuple(restrict(x, values, acc))
 
         blank = jnp.zeros((cy, 128), f32)
-        carry = lax.fori_loop(0, cx, finish, (blank, blank) + clean)
+        carry = planes(0, cx, finish, (blank, blank) + clean, 2)
         gam = jnp.sum(jnp.sum(carry[0], axis=0, keepdims=True), axis=1, keepdims=True)
         ene = jnp.sum(jnp.sum(carry[1], axis=0, keepdims=True), axis=1, keepdims=True)
         push(slot, carry[2:], gam, ene)
@@ -537,7 +549,7 @@
                     out.append(gathered(u, x, acc[c]))
                 return tuple(out)
 
-            acc = lax.fori_loop(0, ex, update, nothing)
+            acc = planes(0, ex, update, nothing, 11)
             send_columns(0, 0, acc)
 
         def advance(x, _):

time: 111 us -> 75.2 us (0.68)
  Pallas kernels: 105 us -> 69.1 us
    pallas_call x1, Pallas kernels: 105 us -> 69.1 us  [body(): pl.pallas_call(functools.partial(kernel, (nx, ny, nz, cx, cy, vectors, or...]
where the time goes in v2:
time: 75.2 us; the launch traced here: 75 us
  Pallas kernels  69.1 us (92%)
  local copies, waits for them, and re-layouts  5.3 us (7%)
    pallas_call x1, Pallas kernels, body(): pl.pallas_call(functools.partial(kernel, (nx, ny, nz, cx, cy, vectors, or...  69.1 us
    unnamed x3, local copies, waits for them, and re-layouts  5.3 us

profile of v2, /device:TPU:0, one launch (start us, length us, event | category | flops | bytes accessed | tf_op | source)
XLA Modules:
  0.0 75.0 jit_solution(3523551166725681292)
XLA Ops:
  0.6 69.1 %shard_map.76 = (f32[3,16,16,128]{3,2,1,0:T(8,128)}, f32[3,16,16,128]{3,2,1,0:T(8,128)}, f32[3,16,16,128]{3,2,1,0:T(8,128)}) custom-call(f32[3,16,16,128]{3,2,1,0:T(8,128)} %forces.1, f32[16,16,128]{2,1,0:T(8,128)} %mass.1, f32[16,3,16,16,128]{4,3,2,1,0:T(8,128)} %defl_hbm.1, f32[256,512]{1,0:T(8,128)} %factor.1, s32[32]{0:T(128)} %slots_hbm.1), custom_call_target="tpu_custom_call" | custom-call | tf_op jit(solution)/shard_map/pallas_call | solution.py:595
  69.7 1.8 %copy.11 = f32[3,16,16,128]{3,2,1,0:T(8,128)} copy(f32[3,16,16,128]{3,2,1,0:T(8,128)} %get-tuple-element.6) | data formatting | bytes 786432
  71.5 1.8 %copy.12 = f32[3,16,16,128]{3,2,1,0:T(8,128)} copy(f32[3,16,16,128]{3,2,1,0:T(8,128)} %get-tuple-element.7) | data formatting | bytes 786432
  73.2 1.8 %copy.13 = f32[3,16,16,128]{3,2,1,0:T(8,128)} copy(f32[3,16,16,128]{3,2,1,0:T(8,128)} %get-tuple-element.8) | data formatting | bytes 786432

commit v3 on v2

--- a/solution.py
+++ b/solution.py
@@ -39,7 +39,7 @@
 def kernel(
     sizes,
     forces, mass, defl_hbm, factor, slots_hbm,
-    sol, res, direc,
+    out,
     zext, rext, idir, cext, cquarter, mext, cor, ua, ub, uz,
     zsend, zgot, edge, fix, cpack, defl,
     full, inv, sol_mat, turned, krows, gsend, gat, gres, gdir, slots,
@@ -48,6 +48,7 @@
 ):
     nx, ny, nz, cx, cy, vectors, order = sizes
     n = nx * ny * nz
+    sol, res, direc = out.at[0], out.at[1], out.at[2]
     ex = cx + 2 * W
     pitch = zext.shape[3]
     tall = up8(cy + 2 * W)
@@ -577,6 +578,15 @@
     lax.fori_loop(0, ITERS, iterate, (one, one))
 
 
+def hand_out(whole, *refs):
+    outs, sems = refs[:-1], refs[-1]
+    copies = [pltpu.make_async_copy(whole.at[i], out, sems.at[i]) for i, out in enumerate(outs)]
+    for copy in copies:
+        copy.start()
+    for copy in copies:
+        copy.wait()
+
+
 def solution(mesh):
     nx, ny, nz = mesh.shape["gx"], mesh.shape["gy"], mesh.shape["gz"]
 
@@ -592,11 +602,12 @@
         field = (3, ex, pitch, 128)
         dma = pltpu.SemaphoreType.DMA
         peers = max(nz - 1, 1)
-        return pl.pallas_call(
+        room = 66 * 1000 * 1000
+        whole = pl.pallas_call(
             functools.partial(kernel, (nx, ny, nz, cx, cy, vectors, order)),
-            out_shape=[jax.ShapeDtypeStruct(forces.shape, f32)] * 3,
+            out_shape=jax.ShapeDtypeStruct((3, *forces.shape), f32),
             in_specs=[pl.BlockSpec(memory_space=pl.ANY)] * 5,
-            out_specs=[pl.BlockSpec(memory_space=pltpu.VMEM)] * 3,
+            out_specs=pl.BlockSpec(memory_space=pltpu.VMEM),
             scratch_shapes=[
                 vm(2, *field), vm(*field), vm(*field), vm(ex, pitch, 128), vm(ex, pitch, 128),
                 vm(1, ex, pitch, 128), vm(*field), vm(*field), vm(*field), vm(*field),
@@ -611,9 +622,17 @@
                 dma((peers,)), dma((peers,)), dma((peers,)), dma((peers,)), dma((5,)),
             ],
             compiler_params=pltpu.CompilerParams(
-                collective_id=0, has_side_effects=True, vmem_limit_bytes=66 * 1000 * 1000
+                collective_id=0, has_side_effects=True, vmem_limit_bytes=room
             ),
         )(forces, mass_shift, deflation, coarse_factor, coarse_slot)
+        return pl.pallas_call(
+            hand_out,
+            out_shape=[jax.ShapeDtypeStruct(forces.shape, f32)] * 3,
+            in_specs=[pl.BlockSpec(memory_space=pltpu.VMEM)],
+            out_specs=[pl.BlockSpec(memory_space=pl.ANY)] * 3,
+            scratch_shapes=[dma((3,))],
+            compiler_params=pltpu.CompilerParams(vmem_limit_bytes=4 * 1000 * 1000),
+        )(whole)
 
     return jax.shard_map(
         body,

time: 75.2 us -> 72.2 us (0.960)
  local copies, waits for them, and re-layouts: 5.3 us -> 1.26 us
  Pallas kernels: 69.1 us -> 70.1 us
    unnamed x3 -> x2, local copies, waits for them, and re-layouts: 5.3 us -> 1.26 us
    pallas_call x0 -> x1, Pallas kernels: none -> 1.03 us  [body(): pl.pallas_call(hand_out, out_shape=[jax.ShapeDtypeStruct(forces.shape, f3...]
where the time goes in v3:
time: 72.2 us; the launch traced here: 72 us
  Pallas kernels  70.1 us (97%)
  local copies, waits for them, and re-layouts  1.26 us (2%)
    pallas_call x1, Pallas kernels, body(): pl.pallas_call(functools.partial(kernel, (nx, ny, nz, cx, cy, vectors, or...  69.1 us

profile of v3, /device:TPU:0, one launch (start us, length us, event | category | flops | bytes accessed | tf_op | source)
XLA Modules:
  0.0 72.0 jit_solution(6914563314761924629)
XLA Ops:
  0.6 69.1 %shard_map.76.whole = f32[3,3,16,16,128]{4,3,2,1,0:T(8,128)} custom-call(f32[3,16,16,128]{3,2,1,0:T(8,128)} %forces.1, f32[16,16,128]{2,1,0:T(8,128)} %mass.1, f32[16,3,16,16,128]{4,3,2,1,0:T(8,128)} %defl_hbm.1, f32[256,512]{1,0:T(8,128)} %factor.1, s32[32]{0:T(128)} %slots_hbm.1), custom_call_target="tpu_custom_call" | custom-call | tf_op jit(solution)/shard_map/pallas_call | solution.py:606
  69.7 0.0 copy-start
  69.7 1.3 %copy-done = f32[3,3,16,16,128]{4,3,2,1,0:T(8,128)S(1)} copy-done((f32[3,3,16,16,128]{4,3,2,1,0:T(8,128)S(1)}, f32[3,3,16,16,128]{4,3,2,1,0:T(8,128)}, u32[]{:S(2)}) %copy-start) | copy-done | bytes 1179672
  71.0 1.0 %shard_map.77 = (f32[3,16,16,128]{3,2,1,0:T(8,128)}, f32[3,16,16,128]{3,2,1,0:T(8,128)}, f32[3,16,16,128]{3,2,1,0:T(8,128)}) custom-call(f32[3,3,16,16,128]{4,3,2,1,0:T(8,128)S(1)} %copy-done), custom_call_target="tpu_custom_call" | custom-call | tf_op jit(solution)/shard_map/pallas_call | solution.py:628
Async XLA Ops:
  69.7 1.3 %copy-start = (f32[3,3,16,16,128]{4,3,2,1,0:T(8,128)S(1)}, f32[3,3,16,16,128]{4,3,2,1,0:T(8,128)}, u32[]{:S(2)}) copy-start(f32[3,3,16,16,128]{4,3,2,1,0:T(8,128)} %shard_map.76.whole) | copy-start | bytes 3538948

commit v4 on v3

--- a/solution.py
+++ b/solution.py
@@ -498,7 +498,7 @@
                     zext[slot, c, x, W + t : W + t + 8] = diag * here[c] - 0.25 * off[c]
             return 0
 
-        planes(W, W + cx, image, 0, 4)
+        planes(W, W + cx, image, 0, 8)
         take_columns(2, 3, False)
 
         def finish(x, carry):
@@ -515,7 +515,7 @@
             return (gam, ene) + tuple(restrict(x, values, acc))
 
         blank = jnp.zeros((cy, 128), f32)
-        carry = planes(0, cx, finish, (blank, blank) + clean, 2)
+        carry = planes(0, cx, finish, (blank, blank) + clean, 4)
         gam = jnp.sum(jnp.sum(carry[0], axis=0, keepdims=True), axis=1, keepdims=True)
         ene = jnp.sum(jnp.sum(carry[1], axis=0, keepdims=True), axis=1, keepdims=True)
         push(slot, carry[2:], gam, ene)

time: 72.2 us -> 70.8 us (0.981)
  Pallas kernels: 70.1 us -> 68.7 us
    pallas_call x1, Pallas kernels: 69.1 us -> 67.7 us  [body(): pl.pallas_call(functools.partial(kernel, (nx, ny, nz, cx, cy, vectors, or...]
where the time goes in v4:
time: 70.8 us; the launch traced here: 70.6 us
  Pallas kernels  68.7 us (97%)
  local copies, waits for them, and re-layouts  1.26 us (2%)
    pallas_call x1, Pallas kernels, body(): pl.pallas_call(functools.partial(kernel, (nx, ny, nz, cx, cy, vectors, or...  67.7 us

profile of v4, /device:TPU:0, one launch (start us, length us, event | category | flops | bytes accessed | tf_op | source)
XLA Modules:
  0.0 70.6 jit_solution(8476611911487563863)
XLA Ops:
  0.6 67.7 %shard_map.76.whole = f32[3,3,16,16,128]{4,3,2,1,0:T(8,128)} custom-call(f32[3,16,16,128]{3,2,1,0:T(8,128)} %forces.1, f32[16,16,128]{2,1,0:T(8,128)} %mass.1, f32[16,3,16,16,128]{4,3,2,1,0:T(8,128)} %defl_hbm.1, f32[256,512]{1,0:T(8,128)} %factor.1, s32[32]{0:T(128)} %slots_hbm.1), custom_call_target="tpu_custom_call" | custom-call | tf_op jit(solution)/shard_map/pallas_call | solution.py:606
  68.3 0.0 copy-start
  68.4 1.3 %copy-done = f32[3,3,16,16,128]{4,3,2,1,0:T(8,128)S(1)} copy-done((f32[3,3,16,16,128]{4,3,2,1,0:T(8,128)S(1)}, f32[3,3,16,16,128]{4,3,2,1,0:T(8,128)}, u32[]{:S(2)}) %copy-start) | copy-done | bytes 1179672
  69.6 1.0 %shard_map.77 = (f32[3,16,16,128]{3,2,1,0:T(8,128)}, f32[3,16,16,128]{3,2,1,0:T(8,128)}, f32[3,16,16,128]{3,2,1,0:T(8,128)}) custom-call(f32[3,3,16,16,128]{4,3,2,1,0:T(8,128)S(1)} %copy-done), custom_call_target="tpu_custom_call" | custom-call | tf_op jit(solution)/shard_map/pallas_call | solution.py:628
Async XLA Ops:
  68.3 1.3 %copy-start = (f32[3,3,16,16,128]{4,3,2,1,0:T(8,128)S(1)}, f32[3,3,16,16,128]{4,3,2,1,0:T(8,128)}, u32[]{:S(2)}) copy-start(f32[3,3,16,16,128]{4,3,2,1,0:T(8,128)} %shard_map.76.whole) | copy-start | bytes 3538948
